TPU v7x, 32 devices: a whole 2x2x4 slice. The times are simulated.
32 devices in a mesh: rep: 2 (over x), exp: 2 (over core), tp: 8 (over z, y).
Axes of the slice: x: 2, y: 2, z: 4, core: 2. Of those that a mesh axis runs over, the one named last changes fastest.
Arguments:
- tokens: bfloat16 [1024, 4096], P(('rep', 'exp'), 'tp'), parts along dimension 0
- smooth_in: float32 [4096], P('tp'), may hold values from 0.5 to 2
- expert_ids: int32 [1024, 2], P(('rep', 'exp')), parts along dimension 0, may hold values from 0 to 3, as said below
- gate_fixed: int32 [1024, 2], P(('rep', 'exp')), parts along dimension 0, may hold values from 1 to 32767
- slots: int32 [1024, 2], P(('rep', 'exp')), parts along dimension 0, may hold values from 0 to 255, as said below
- w_gate: bfloat16 [4, 4096, 7168], P('exp', None, 'tp')
- w_up: bfloat16 [4, 4096, 7168], P('exp', None, 'tp')
- w_down: bfloat16 [4, 7168, 4096], P('exp', 'tp')
- gate_scale: float32 [4, 7168], P('exp', 'tp'), may hold values from 0.00010557433 to 0.0004222973
- up_scale: float32 [4, 7168], P('exp', 'tp'), may hold values from 0.00010557433 to 0.0004222973
- smooth_mid: float32 [4, 7168], P('exp', 'tp'), may hold values from 0.5 to 2
- down_scale: float32 [4, 4096], P('exp'), may hold values from 0.00015961338 to 0.0006384535
Outputs:
- moe_out: bfloat16 [1024, 4096], P(('rep', 'exp'), 'tp'), parts along dimension 0
There are 2 independent parts, one for each index of `rep`. A program takes and returns all parts, laid end to end along the dimension named above; an argument that names none is the same for every part. Nothing has to cross between parts.
Inputs may be any that keep to these rules, and one draw needn't show every extreme that they name: `expert_ids`: the two experts of a token differ. Within one aligned block of 256 tokens (the tokens of one index of exp), the slots of the pairs that name one expert are distinct and run from 0 to their number less one. In every block some expert is named by 192 or more tokens.
All inputs are finite; a program needn't handle non-finite values.
Results may differ from a plain program's by a relative error of at most 0.006.
Values may be sent and summed in bfloat16 or wider, within the bound.
A program may use at most 128 MiB of HBM per device.

v0:
```python
import jax
import jax.numpy as jnp
from jax import lax
from jax.sharding import PartitionSpec as P

CLIP_RATIO = 0.35
EPSILON = 1e-06


def per_device(
    tokens,
    smooth_in,
    expert_ids,
    gate_fixed,
    slots,
    w_gate,
    w_up,
    w_down,
    gate_scale,
    up_scale,
    smooth_mid,
    down_scale,
):
    n_groups = lax.axis_size("exp")
    local_experts = w_gate.shape[0]
    block_rows = tokens.shape[0]
    capacity = 3 * block_rows // 4
    rows_all = local_experts * n_groups * capacity
    smoothed = tokens.astype(jnp.float32) / smooth_in[None, :]
    local_peak = jnp.max(jnp.abs(smoothed), axis=1)
    row_peak_value = lax.pmax(local_peak, "tp")
    in_scale = CLIP_RATIO * (row_peak_value + EPSILON) / 127.0
    quantized = jnp.clip(smoothed / in_scale[:, None], -127.0, 127.0).astype(jnp.bfloat16)
    gate_values = gate_fixed.astype(jnp.float32)
    weight = gate_values / jnp.sum(gate_values, axis=1, keepdims=True)
    kept_pairs = slots < capacity
    target = expert_ids * capacity + jnp.minimum(slots, capacity - 1)
    positions = jnp.arange(rows_all, dtype=jnp.int32)
    place_first = (target[:, 0][None, :] == positions[:, None]) & kept_pairs[:, 0][None, :]
    place_second = (target[:, 1][None, :] == positions[:, None]) & kept_pairs[:, 1][None, :]
    placement_map = place_first | place_second
    send_rows = jnp.dot(
        placement_map.astype(jnp.bfloat16), quantized, preferred_element_type=jnp.float32
    ).astype(jnp.bfloat16)
    send_rows = send_rows.reshape(n_groups, local_experts, capacity, tokens.shape[1])
    scale_slots = jnp.sum(jnp.where(placement_map, in_scale[None, :], 0.0), axis=1).reshape(
        n_groups, local_experts, capacity
    )
    recv_rows = lax.all_to_all(send_rows, "exp", split_axis=0, concat_axis=0, tiled=True)
    recv_scale = lax.all_to_all(scale_slots, "exp", split_axis=0, concat_axis=0, tiled=True)
    arrived = lax.all_gather(recv_rows, "tp", axis=3, tiled=True)
    gate_more = jnp.einsum("secl,elf->secf", arrived, w_gate, preferred_element_type=jnp.float32)
    up_more = jnp.einsum("secl,elf->secf", arrived, w_up, preferred_element_type=jnp.float32)
    gate_pre = gate_more * recv_scale[..., None] * gate_scale[None, :, None, :]
    up_pre = up_more * recv_scale[..., None] * up_scale[None, :, None, :]
    hidden = jax.nn.silu(gate_pre) * up_pre / smooth_mid[None, :, None, :]
    hidden_max = lax.pmax(jnp.max(jnp.abs(hidden), axis=3), "tp")
    mid_scale = CLIP_RATIO * (hidden_max + EPSILON) / 127.0
    hidden_q = jnp.clip(hidden / mid_scale[..., None], -127.0, 127.0).astype(jnp.bfloat16)
    down_acc = jnp.einsum("secf,efd->secd", hidden_q, w_down, preferred_element_type=jnp.float32)
    partial_value = down_acc * mid_scale[..., None] * down_scale[None, :, None, :]
    summed = lax.psum_scatter(partial_value, "tp", scatter_dimension=3, tiled=True)
    returned = lax.all_to_all(summed, "exp", split_axis=0, concat_axis=0, tiled=True)
    slot_table = returned.reshape(rows_all, returned.shape[3])
    picked = jnp.take(slot_table, target, axis=0)
    pair_weight = jnp.where(kept_pairs, weight, 0.0)
    combined = jnp.sum(picked * pair_weight[:, :, None], axis=1)
    return combined.astype(jnp.bfloat16)


def solution(mesh):
    in_specs = (
        P(("rep", "exp"), "tp"),
        P("tp"),
        P(("rep", "exp"), None),
        P(("rep", "exp"), None),
        P(("rep", "exp"), None),
        P("exp", None, "tp"),
        P("exp", None, "tp"),
        P("exp", "tp", None),
        P("exp", "tp"),
        P("exp", "tp"),
        P("exp", "tp"),
        P("exp", None),
    )
    out_specs = P(("rep", "exp"), "tp")
    return jax.shard_map(
        per_device, mesh=mesh, in_specs=in_specs, out_specs=out_specs, check_vma=False
    )
```

profile of v0, /device:TPU:0, one launch (start us, length us, event | category | flops | bytes accessed | tf_op | source)
XLA Modules:
  0.0 419.6 jit_solution(16711710052682556564)
XLA Ops:
  6.5 0.0 all-gather.2.cloned.1.call-start
  6.5 0.7 compare_and_fusion
  7.3 0.7 convert_reduce_fusion
  8.0 0.7 divide_select_fusion
  8.7 1.1 fusion.24
  9.8 23.2 %pmax.14 = f32[256]{0:T(256)S(1)} all-reduce(f32[256]{0:T(256)S(1)} %fusion.24), channel_id=1, replica_groups=mesh['rep'=2,'exp'=2,'tp'=8] {'tp'}, use_global_device_ids=true, to_apply=%region_1.0 | all-reduce | flops 256 | bytes 2048 | tf_op jit(solution)/shard_map/pmax | solution.py:31
  33.0 1.5 convolution_convert_fusion
  34.5 4.4 %all_to_all.15 = bf16[2,2,192,512]{3,2,1,0:T(8,128)(2,1)S(1)} all-to-all(bf16[2,2,192,512]{3,2,1,0:T(8,128)(2,1)S(1)} %bitcast.44), channel_id=1, replica_groups=mesh['rep'=2,'exp'=2,'tp'=8] {'exp'}, dimensions={0} | all-to-all | bytes 1572864 | tf_op jit(solution)/shard_map/all_to_all | solution.py:49
  38.8 0.9 copy.29
  39.8 0.0 all-gather.2.cloned.1.call-update
  39.8 0.0 reduce-scatter.2.cloned.1.call-start
  39.8 0.3 select_reduce_fusion
  40.2 0.1 reshape.30
  40.3 3.7 all_to_all.16
  44.0 92.7 %all-gather.2.cloned.1.call-done = bf16[2,2,192,4096]{3,2,0,1:T(8,128)(2,1)} async-done(((bf16[2,2,192,512]{3,2,0,1:T(8,128)(2,1)}), bf16[2,2,192,4096]{3,2,0,1:T(8,128)(2,1)}) %all-gather.2.cloned.1.call-update) | async-done | bytes 6291472 | tf_op jit(solution)/shard_map/all_gather | solution.py:51
  136.7 14.6 %fusion.2 = f32[2,2,192,896]{3,2,1,0:T(8,128)S(1)} fusion(bf16[2,2,192,4096]{3,2,0,1:T(8,128)(2,1)} %all-gather.2.cloned.1.call-done, bf16[2,4096,896]{2,1,0:T(8,128)(2,1)} %param.18), kind=kOutput, calls=%fused_computation.3 | convolution fusion | flops 5637144576 | bytes 23724032 | tf_op jit(solution)/shard_map/secl,elf->secf/dot_general | solution.py:53
  151.3 0.0 copy-done.2
  151.3 0.0 copy-start.1
  151.3 10.8 %abs_reduce_fusion = (f32[2,2,192]{2,0,1:T(2,128)S(1)}, f32[2,2,192,896]{3,2,0,1:T(8,128)S(1)}) fusion(f32[2,896]{1,0:T(2,128)S(1)} %copy-done.4, f32[2,896]{1,0:T(2,128)S(1)} %copy-done.2, f32[2,2,192,896]{3,2,1,0:T(8,128)S(1)} %fusion.2, f32[2,896]{1,0:T(2,128)S(1)} %copy-done.3, f32[2,2,192]{2,0,1:T(2,128)S(1)} %copy.30, ...), kind=kOutput, calls=%fused_computation.15 | convolution fusion | flops 5645401088 | bytes 26504192 | tf_op jit(solution)/shard_map/secl,elf->secf/dot_general | solution.py:52
  162.2 18.8 %pmax.15 = f32[2,2,192]{2,0,1:T(2,128)S(1)} all-reduce(f32[2,2,192]{2,0,1:T(2,128)S(1)} %get-tuple-element.13), channel_id=1, replica_groups=mesh['rep'=2,'exp'=2,'tp'=8] {'tp'}, use_global_device_ids=true, to_apply=%region_4.5 | all-reduce | flops 768 | bytes 6144 | tf_op jit(solution)/shard_map/pmax | solution.py:57
  181.0 14.8 %fusion.6 = f32[2,2,192,4096]{3,2,0,1:T(8,128)} fusion(bf16[2,896,4096]{2,1,0:T(8,128)(2,1)} %param.19, f32[2,4096]{1,0:T(2,128)S(1)} %copy-done.1, f32[2,2,192]{2,0,1:T(2,128)S(1)} %add_multiply_fusion, f32[2,2,192,896]{3,2,0,1:T(8,128)S(1)} %get-tuple-element.14, f32[2,896]{1,0:T(2,128)S(1)} %copy-done.4), kind=kOutput, calls=%fused_computation.8 | convolution fusion | flops 5646188544 | bytes 30058496 | tf_op jit(solution)/shard_map/secf,efd->secd/dot_general | solution.py:60
  195.8 0.0 reduce-scatter.2.cloned.1.call-update
  195.8 0.1 copy.32
  196.0 0.1 reshape.34
  196.1 0.1 copy.33
  196.2 0.2 copy.28
  196.4 204.7 %reduce-scatter.2.cloned.1.call-done = f32[2,2,192,512]{3,2,0,1:T(8,128)} async-done(((f32[2,2,192,4096]{3,2,0,1:T(8,128)}), f32[2,2,192,512]{3,2,0,1:T(8,128)}) %reduce-scatter.2.cloned.1.call-update) | async-done | bytes 1572880 | tf_op jit(solution)/shard_map/reduce_scatter | solution.py:62
  401.1 1.5 copy.31
  402.6 5.0 %all_to_all.17 = f32[2,2,192,512]{3,2,1,0:T(8,128)S(1)} all-to-all(f32[2,2,192,512]{3,2,1,0:T(8,128)S(1)} %copy.31), channel_id=1, replica_groups=mesh['rep'=2,'exp'=2,'tp'=8] {'exp'}, dimensions={0} | all-to-all | bytes 3145728 | tf_op jit(solution)/shard_map/all_to_all | solution.py:63
  407.6 1.6 gather_fusion
  409.3 0.6 reshape.33
  409.9 2.9 multiply_reduce_fusion
  (15 shorter events, 0.1 us)
Async XLA Ops:
  6.5 130.1 %all-gather.2.cloned.1.call-start = ((), (), s32[]{:S(2)}) async-start(), calls=%async_computation.4 | async-start | bytes 7077888 | tf_op jit(solution)/shard_map/all_gather | solution.py:51
  39.8 361.3 %reduce-scatter.2.cloned.1.call-start = ((), (), s32[]{:S(2)}) async-start(), calls=%async_computation.5 | async-start | bytes 14155776 | tf_op jit(solution)/shard_map/reduce_scatter | solution.py:62
  43.9 107.3 %copy-start.2 = (f32[2,896]{1,0:T(2,128)S(1)}, f32[2,896]{1,0:T(2,128)}, u32[]{:S(2)}) copy-start(f32[2,896]{1,0:T(2,128)} %param.21) | copy-start | bytes 21508
  43.9 107.4 %copy-start.3 = (f32[2,896]{1,0:T(2,128)S(1)}, f32[2,896]{1,0:T(2,128)}, u32[]{:S(2)}) copy-start(f32[2,896]{1,0:T(2,128)} %param.20) | copy-start | bytes 21508
  44.0 107.4 %copy-start.4 = (f32[2,896]{1,0:T(2,128)S(1)}, f32[2,896]{1,0:T(2,128)}, u32[]{:S(2)}) copy-start(f32[2,896]{1,0:T(2,128)} %param.22) | copy-start | bytes 21508
  136.7 14.6 %copy-start = (bf16[2,2,192,4096]{3,2,0,1:T(8,128)(2,1)S(1)}, bf16[2,2,192,4096]{3,2,0,1:T(8,128)(2,1)}, u32[]{:S(2)}) copy-start(bf16[2,2,192,4096]{3,2,0,1:T(8,128)(2,1)} %all-gather.2.cloned.1.call-done) | copy-start | bytes 18874372
  151.3 29.6 %copy-start.1 = (f32[2,4096]{1,0:T(2,128)S(1)}, f32[2,4096]{1,0:T(2,128)}, u32[]{:S(2)}) copy-start(f32[2,4096]{1,0:T(2,128)} %param.23) | copy-start | bytes 98308
Sparse Core Ops, SparseCore 0:
  39.9 96.7 all-gather.1
  195.9 205.1 reduce-scatter.1
where the time goes:
time: 420 us
  waiting for transfers between devices  297 us (71%)
  blocking collectives  55 us (13%)
  matrix products  41.7 us (10%)
  between operations  13.6 us (3%)
  other arithmetic  6.44 us (2%)
  local copies, waits for them, and re-layouts  5.43 us (1%)
    reduce_scatter x1, waiting for transfers between devices, per_device(): lax.psum_scatter(partial_value, 'tp', scatter_dimension=3, tiled=True)  205 us
    all_gather x1, waiting for transfers between devices, per_device(): arrived = lax.all_gather(recv_rows, 'tp', axis=3, tiled=True)  92.7 us
    pmax x1, blocking collectives, per_device(): row_peak_value = lax.pmax(local_peak, 'tp')  23.2 us
    pmax x1, blocking collectives, per_device(): hidden_max = lax.pmax(jnp.max(jnp.abs(hidden), axis=3), 'tp')  18.8 us
    dot_general x1, matrix products, per_device(): jnp.einsum('secf,efd->secd', hidden_q, w_down, preferred_element_type=jnp...  14.8 us
    dot_general x1, matrix products, per_device(): jnp.einsum('secl,elf->secf', arrived, w_up, preferred_element_type=jnp.fl...  14.6 us
    dot_general x1, matrix products, per_device(): jnp.einsum('secl,elf->secf', arrived, w_gate, preferred_element_type=jnp....  10.8 us
  transfers between devices with their start and end apart: 2, of which 2 were waited for; matrix products, arithmetic and copies ran while one was open for 0% of the time, Pallas kernels for 0%

commit v1 on v0

--- a/solution.py
+++ b/solution.py
@@ -5,6 +5,10 @@
 
 CLIP_RATIO = 0.35
 EPSILON = 1e-06
+
+
+def close_results(point, dim_no, mesh_dim):
+    return jnp.concatenate(lax.all_gather(point, mesh_dim), axis=dim_no)
 
 
 def per_device(
@@ -48,7 +52,7 @@
     )
     recv_rows = lax.all_to_all(send_rows, "exp", split_axis=0, concat_axis=0, tiled=True)
     recv_scale = lax.all_to_all(scale_slots, "exp", split_axis=0, concat_axis=0, tiled=True)
-    arrived = lax.all_gather(recv_rows, "tp", axis=3, tiled=True)
+    arrived = close_results(recv_rows, 3, "tp")
     gate_more = jnp.einsum("secl,elf->secf", arrived, w_gate, preferred_element_type=jnp.float32)
     up_more = jnp.einsum("secl,elf->secf", arrived, w_up, preferred_element_type=jnp.float32)
     gate_pre = gate_more * recv_scale[..., None] * gate_scale[None, :, None, :]

time: 420 us -> 439 us (1.045)
  local copies, waits for them, and re-layouts: 5.43 us -> 23.9 us
    reshape x0 -> x1, local copies, waits for them, and re-layouts: none -> 10.4 us  [close_results(): return jnp.concatenate(lax.all_gather(point, mesh_dim), axis=dim_no)]
    all_gather x0 -> x1, local copies, waits for them, and re-layouts: none -> 9.02 us  [close_results(): return jnp.concatenate(lax.all_gather(point, mesh_dim), axis=dim_no)]
where the time goes in v1:
time: 439 us; the launch traced here: 438 us
  waiting for transfers between devices  297 us (68%)
  blocking collectives  55.7 us (13%)
  matrix products  41.8 us (10%)
  local copies, waits for them, and re-layouts  23.9 us (5%)
  between operations  13.6 us (3%)
  other arithmetic  6.44 us (1%)
    reduce_scatter x1, waiting for transfers between devices, per_device(): lax.psum_scatter(partial_value, 'tp', scatter_dimension=3, tiled=True)  205 us
    all_gather x1, waiting for transfers between devices, close_results(): return jnp.concatenate(lax.all_gather(point, mesh_dim), axis=dim_no)  91.9 us
    pmax x1, blocking collectives, per_device(): row_peak_value = lax.pmax(local_peak, 'tp')  23.2 us
    pmax x1, blocking collectives, per_device(): hidden_max = lax.pmax(jnp.max(jnp.abs(hidden), axis=3), 'tp')  18.7 us
    dot_general x1, matrix products, per_device(): jnp.einsum('secf,efd->secd', hidden_q, w_down, preferred_element_type=jnp...  14.8 us
    dot_general x1, matrix products, per_device(): jnp.einsum('secl,elf->secf', arrived, w_up, preferred_element_type=jnp.fl...  14.6 us
    dot_general x1, matrix products, per_device(): jnp.einsum('secl,elf->secf', arrived, w_gate, preferred_element_type=jnp....  10.8 us
    reshape x1, local copies, waits for them, and re-layouts, close_results(): return jnp.concatenate(lax.all_gather(point, mesh_dim), axis=dim_no)  10.4 us
  transfers between devices with their start and end apart: 2, of which 2 were waited for; matrix products, arithmetic and copies ran while one was open for 0% of the time, Pallas kernels for 0%

profile of v1, /device:TPU:0, one launch (start us, length us, event | category | flops | bytes accessed | tf_op | source)
XLA Modules:
  0.0 438.1 jit_solution(9500382347376542037)
XLA Ops:
  6.5 0.0 all-gather.3.cloned.1.call-start
  6.5 0.7 compare_and_fusion
  7.3 0.7 convert_reduce_fusion
  8.0 0.7 divide_select_fusion
  8.7 1.1 fusion.24
  9.8 23.2 %pmax.14 = f32[256]{0:T(256)S(1)} all-reduce(f32[256]{0:T(256)S(1)} %fusion.24), channel_id=1, replica_groups=mesh['rep'=2,'exp'=2,'tp'=8] {'tp'}, use_global_device_ids=true, to_apply=%region_1.0 | all-reduce | flops 256 | bytes 2048 | tf_op jit(solution)/shard_map/pmax | solution.py:35
  33.0 1.5 convolution_convert_fusion
  34.5 5.2 %all_to_all.15 = bf16[2,2,192,512]{3,2,1,0:T(8,128)(2,1)} all-to-all(bf16[2,2,192,512]{3,2,1,0:T(8,128)(2,1)S(1)} %bitcast.54), channel_id=1, replica_groups=mesh['rep'=2,'exp'=2,'tp'=8] {'exp'}, dimensions={0} | all-to-all | bytes 1572864 | tf_op jit(solution)/shard_map/all_to_all | solution.py:53
  39.6 0.0 all-gather.3.cloned.1.call-update
  39.6 0.0 reduce-scatter.2.cloned.1.call-start
  39.7 0.3 select_reduce_fusion
  40.0 0.1 reshape.38
  40.1 3.7 all_to_all.16
  43.8 91.9 %all-gather.3.cloned.1.call-done = bf16[16,2,192,512]{3,2,1,0:T(8,128)(2,1)} async-done(((bf16[2,2,192,512]{3,2,1,0:T(8,128)(2,1)}), bf16[16,2,192,512]{3,2,1,0:T(8,128)(2,1)}) %all-gather.3.cloned.1.call-update) | async-done | bytes 6291472 | tf_op jit(solution)/shard_map/all_gather | solution.py:11
  135.7 9.0 %copy.38 = bf16[8,2,2,192,512]{4,0,3,1,2:T(8,128)(2,1)} copy(bf16[8,2,2,192,512]{4,3,2,1,0:T(8,128)(2,1)} %bitcast.53) | data formatting | bytes 12582912 | tf_op jit(solution)/shard_map/all_gather | solution.py:11
  144.8 10.4 %reshape.37 = bf16[2,2,192,4096]{3,2,0,1:T(8,128)(2,1)} reshape(bf16[2,2,192,8,512]{4,3,2,0,1:T(8,128)(2,1)} %bitcast.52) | data formatting | bytes 12582912 | tf_op jit(solution)/shard_map/reshape | solution.py:11
  155.2 14.6 %fusion.2 = f32[2,2,192,896]{3,2,1,0:T(8,128)S(1)} fusion(bf16[2,2,192,4096]{3,2,0,1:T(8,128)(2,1)} %reshape.37, bf16[2,4096,896]{2,1,0:T(8,128)(2,1)} %param.18), kind=kOutput, calls=%fused_computation.3 | convolution fusion | flops 5637144576 | bytes 23724032 | tf_op jit(solution)/shard_map/secl,elf->secf/dot_general | solution.py:57
  169.9 0.0 copy-start.1
  169.9 10.8 %abs_reduce_fusion = (f32[2,2,192]{2,0,1:T(2,128)S(1)}, f32[2,2,192,896]{3,2,0,1:T(8,128)S(1)}) fusion(f32[2,896]{1,0:T(2,128)S(1)} %copy-done.4, f32[2,896]{1,0:T(2,128)S(1)} %copy-done.2, f32[2,2,192,896]{3,2,1,0:T(8,128)S(1)} %fusion.2, f32[2,896]{1,0:T(2,128)S(1)} %copy-done.3, f32[2,2,192]{2,0,1:T(2,128)S(1)} %copy.30, ...), kind=kOutput, calls=%fused_computation.16 | convolution fusion | flops 5645401088 | bytes 26504192 | tf_op jit(solution)/shard_map/secl,elf->secf/dot_general | solution.py:56
  180.7 18.7 %pmax.15 = f32[2,2,192]{2,0,1:T(2,128)S(1)} all-reduce(f32[2,2,192]{2,0,1:T(2,128)S(1)} %get-tuple-element.13), channel_id=1, replica_groups=mesh['rep'=2,'exp'=2,'tp'=8] {'tp'}, use_global_device_ids=true, to_apply=%region_4.5 | all-reduce | flops 768 | bytes 6144 | tf_op jit(solution)/shard_map/pmax | solution.py:61
  199.5 14.8 %fusion.6 = f32[2,2,192,4096]{3,2,0,1:T(8,128)} fusion(bf16[2,896,4096]{2,1,0:T(8,128)(2,1)} %param.19, f32[2,4096]{1,0:T(2,128)S(1)} %copy-done.1, f32[2,2,192]{2,0,1:T(2,128)S(1)} %add_multiply_fusion, f32[2,2,192,896]{3,2,0,1:T(8,128)S(1)} %get-tuple-element.14, f32[2,896]{1,0:T(2,128)S(1)} %copy-done.4), kind=kOutput, calls=%fused_computation.8 | convolution fusion | flops 5646188544 | bytes 30058496 | tf_op jit(solution)/shard_map/secf,efd->secd/dot_general | solution.py:64
  214.3 0.0 reduce-scatter.2.cloned.1.call-update
  214.3 0.1 copy.32
  214.5 0.1 reshape.42
  214.6 0.1 copy.33
  214.8 0.2 copy.28
  215.0 204.6 %reduce-scatter.2.cloned.1.call-done = f32[2,2,192,512]{3,2,0,1:T(8,128)} async-done(((f32[2,2,192,4096]{3,2,0,1:T(8,128)}), f32[2,2,192,512]{3,2,0,1:T(8,128)}) %reduce-scatter.2.cloned.1.call-update) | async-done | bytes 1572880 | tf_op jit(solution)/shard_map/reduce_scatter | solution.py:66
  419.6 1.5 copy.31
  421.1 5.0 %all_to_all.17 = f32[2,2,192,512]{3,2,1,0:T(8,128)S(1)} all-to-all(f32[2,2,192,512]{3,2,1,0:T(8,128)S(1)} %copy.31), channel_id=1, replica_groups=mesh['rep'=2,'exp'=2,'tp'=8] {'exp'}, dimensions={0} | all-to-all | bytes 3145728 | tf_op jit(solution)/shard_map/all_to_all | solution.py:67
  426.1 1.6 gather_fusion
  427.7 0.6 reshape.41
  428.3 2.9 multiply_reduce_fusion
  (16 shorter events, 0.1 us)
Async XLA Ops:
  6.5 129.2 %all-gather.3.cloned.1.call-start = ((), (), s32[]{:S(2)}) async-start(), calls=%async_computation.5 | async-start | bytes 7077888 | tf_op jit(solution)/shard_map/all_gather | solution.py:11
  39.6 379.9 %reduce-scatter.2.cloned.1.call-start = ((), (), s32[]{:S(2)}) async-start(), calls=%async_computation.4 | async-start | bytes 14155776 | tf_op jit(solution)/shard_map/reduce_scatter | solution.py:66
  155.2 14.6 %copy-start = (bf16[2,2,192,4096]{3,2,0,1:T(8,128)(2,1)S(1)}, bf16[2,2,192,4096]{3,2,0,1:T(8,128)(2,1)}, u32[]{:S(2)}) copy-start(bf16[2,2,192,4096]{3,2,0,1:T(8,128)(2,1)} %reshape.37) | copy-start | bytes 18874372
  155.2 14.6 %copy-start.2 = (f32[2,896]{1,0:T(2,128)S(1)}, f32[2,896]{1,0:T(2,128)}, u32[]{:S(2)}) copy-start(f32[2,896]{1,0:T(2,128)} %param.21) | copy-start | bytes 21508
  155.2 14.7 %copy-start.3 = (f32[2,896]{1,0:T(2,128)S(1)}, f32[2,896]{1,0:T(2,128)}, u32[]{:S(2)}) copy-start(f32[2,896]{1,0:T(2,128)} %param.20) | copy-start | bytes 21508
  155.2 14.7 %copy-start.4 = (f32[2,896]{1,0:T(2,128)S(1)}, f32[2,896]{1,0:T(2,128)}, u32[]{:S(2)}) copy-start(f32[2,896]{1,0:T(2,128)} %param.22) | copy-start | bytes 21508
  169.9 29.6 %copy-start.1 = (f32[2,4096]{1,0:T(2,128)S(1)}, f32[2,4096]{1,0:T(2,128)}, u32[]{:S(2)}) copy-start(f32[2,4096]{1,0:T(2,128)} %param.23) | copy-start | bytes 98308
Sparse Core Ops, SparseCore 0:
  39.8 95.9 all-gather.2
  214.5 205.0 reduce-scatter.1
